TPU v7x, 1024 devices: a whole 4x8x16 slice. The times are simulated.
1024 devices in a mesh: edp: 16 (over z), ep: 64 (over y, x, core).
Axes of the slice: x: 4, y: 8, z: 16, core: 2. Of those that a mesh axis runs over, the one named last changes fastest.
Arguments:
- out_grad: bfloat16 [131072, 3584], P(('edp', 'ep')), may hold values from -0.59765625 to 0.59765625
- routes: int32 [131072, 8], P(('edp', 'ep')), may hold values from 0 to 383, as said below
- gate_weights: float32 [131072, 8], P(('edp', 'ep')), may hold values from 0.02 to 0.5
- hidden: bfloat16 [8192, 16384], P('edp', 'ep'), may hold values from -6 to 6
Outputs:
- weight_grad: float32 [3584, 16384], P('edp', 'ep')
Inputs may be any that keep to these rules, and one draw needn't show every extreme that they name: `routes`: each token names 8 different experts, at most one of them below 8. Among the tokens of one device no expert below 8 is named more than 8 times, and on every device one such expert, the same on all, is named exactly 8 times.
All inputs are finite; a program needn't handle non-finite values.
Results may differ from a plain program's by a relative error of at most 0.0029.
Values may be sent and summed in bfloat16 or wider, within the bound.
No kernel may reach another device: no remote copies, remote signals or barrier semaphores. Data moves between devices by JAX's collectives and lax.ppermute only.
A program may use at most 32 MiB of HBM per device.

v0:
```python
import jax
import jax.numpy as jnp
from jax import lax
from jax.experimental import pallas as pl
from jax.experimental.pallas import tpu as pltpu
from jax.sharding import Mesh, PartitionSpec as P

CAP = 8
EXPERTS = 8
GROUP = 4


def place_kernel(grad_in, routes_in, gates_in, out_ref, grad_ref, routes_ref, gates_ref, arrived):
    moves = [
        pltpu.make_async_copy(routes_in, routes_ref, arrived.at[0]),
        pltpu.make_async_copy(gates_in, gates_ref, arrived.at[1]),
        pltpu.make_async_copy(grad_in, grad_ref, arrived.at[2]),
    ]
    for move in moves:
        move.start()
    tokens, features = grad_ref.shape
    moves[0].wait()
    moves[1].wait()
    block = features // (GROUP * GROUP)
    routes = routes_ref[...]
    local = routes < EXPERTS
    weight = jnp.sum(jnp.where(local, gates_ref[...], 0.0), axis=0, keepdims=True)
    weight = jnp.transpose(jnp.broadcast_to(weight, (8, tokens)))[:, :1]
    expert = jnp.sum(jnp.where(local, routes + 1, 0), axis=0, keepdims=True) - 1
    onehot = expert == lax.broadcasted_iota(jnp.int32, (EXPERTS, tokens), 0)
    earlier = lax.broadcasted_iota(jnp.int32, (tokens, tokens), 0) < lax.broadcasted_iota(
        jnp.int32, (tokens, tokens), 1
    )
    ranks = jnp.dot(
        onehot.astype(jnp.float32).astype(jnp.bfloat16),
        earlier.astype(jnp.float32).astype(jnp.bfloat16),
        preferred_element_type=jnp.float32,
    )
    rank = jnp.sum(jnp.where(onehot, ranks, 0.0), axis=0, keepdims=True).astype(jnp.int32)
    slot = jnp.where(expert >= 0, expert * CAP + rank, -1)
    placer = (slot == lax.broadcasted_iota(jnp.int32, (EXPERTS * CAP, tokens), 0)).astype(
        jnp.float32
    ).astype(jnp.bfloat16)
    moves[2].wait()
    routed = (grad_ref[...].astype(jnp.float32) * weight).astype(jnp.bfloat16)
    placed = jnp.dot(placer, routed, preferred_element_type=jnp.float32)
    for low in range(GROUP):
        picked = jnp.concatenate(
            [
                placed[:, (high * GROUP + low) * block : (high * GROUP + low + 1) * block]
                for high in range(GROUP)
            ],
            axis=1,
        )
        out_ref[low] = picked.astype(jnp.bfloat16).reshape(EXPERTS, CAP, GROUP * block)


def place_rows(out_grad, routes, gate_weights):
    features = out_grad.shape[1]
    return pl.pallas_call(
        place_kernel,
        out_shape=jax.ShapeDtypeStruct(
            (GROUP, EXPERTS, CAP, features // GROUP), jnp.bfloat16
        ),
        in_specs=[pl.BlockSpec(memory_space=pltpu.HBM)] * 3,
        scratch_shapes=[
            pltpu.VMEM(out_grad.shape, out_grad.dtype),
            pltpu.VMEM(routes.shape[::-1], routes.dtype),
            pltpu.VMEM(gate_weights.shape[::-1], gate_weights.dtype),
            pltpu.SemaphoreType.DMA((3,)),
        ],
        cost_estimate=pl.CostEstimate(
            flops=2 * 64 * 128 * features, bytes_accessed=3 * 64 * 2 * features, transcendentals=0
        ),
    )(out_grad, routes.T, gate_weights.T)


def gradient(out_grad, routes, gate_weights, hidden):
    columns = hidden.shape[1]
    low, core = lax.axis_index("zl"), lax.axis_index("c")
    outbound = place_rows(out_grad, routes, gate_weights)
    features = outbound.shape[-1]
    outbound = outbound.reshape(GROUP * EXPERTS, CAP, features)
    arrived = lax.all_to_all(outbound, ("zl", "y"), split_axis=0, concat_axis=0, tiled=True)
    mine = hidden.reshape(EXPERTS, GROUP, 2, CAP, columns).transpose(2, 1, 0, 3, 4)
    mine = mine.reshape(2, GROUP, EXPERTS * CAP, columns)
    gathered = [mine]
    for step in (1, 2, 3):
        gathered.append(lax.ppermute(mine, "zl", [(i, i ^ step) for i in range(GROUP)]))
    stacked = jnp.stack(gathered)
    saved = jnp.stack(
        [lax.dynamic_index_in_dim(stacked, low ^ source, 0, False) for source in range(GROUP)],
        axis=2,
    )
    saved = saved.reshape(2, -1, columns)

    arrived = jnp.broadcast_to(
        arrived.reshape(1, -1, features), (GROUP, GROUP * EXPERTS * CAP, features)
    )
    rows = lax.all_to_all(arrived, "x", split_axis=0, concat_axis=0, tiled=True)
    rows = rows.reshape(-1, features)
    others = lax.ppermute(rows, "c", [(0, 1), (1, 0)])

    def product(part, which):
        return lax.dot_general(
            part,
            lax.dynamic_index_in_dim(saved, which, 0, False),
            (((0,), (0,)), ((), ())),
            preferred_element_type=jnp.float32,
        )

    partial = lax.optimization_barrier(product(rows, core))
    partial = partial + product(others, 1 - core)
    partial = partial.astype(jnp.bfloat16).reshape(GROUP, features // GROUP, columns)
    high = lax.axis_index("zh")

    def chunk(step):
        return lax.dynamic_index_in_dim(partial, high ^ step, 0, False)

    total = chunk(0).astype(jnp.float32)
    for step in (2, 3, 1):
        got = lax.ppermute(chunk(step), "zh", [(i, i ^ step) for i in range(GROUP)])
        total = total + got.astype(jnp.float32)
    return total


def solution(mesh):
    axes = ("zh", "zl", "y", "x", "c")
    fine = Mesh(mesh.devices.reshape(GROUP, GROUP, EXPERTS, 4, 2), axes)
    tokens = P(axes, None)
    return jax.shard_map(
        gradient,
        mesh=fine,
        in_specs=(tokens, tokens, tokens, P(("zh", "zl"), ("y", "x", "c"))),
        out_specs=P(("zh", "zl"), ("y", "x", "c")),
        check_vma=False,
    )
```

profile of v0, /device:TPU:1, one launch (start us, length us, event | category | flops | bytes accessed | tf_op | source)
XLA Modules:
  0.0 128.5 jit_solution(11495858240898977727)
XLA Ops:
  0.0 2.4 %shard_map.46 = bf16[4,8,8,896]{3,2,1,0:T(8,128)(2,1)} custom-call(bf16[128,3584]{1,0:T(8,128)(2,1)} %grad_in.1, s32[8,128]{1,0:T(8,128)} %bitcast.59, f32[8,128]{1,0:T(8,128)} %bitcast.60), custom_call_target="tpu_custom_call" | custom-call | flops 58720256 | bytes 1376256 | tf_op jit(solution)/shard_map/pallas_call | solution.py:60
  2.4 25.5 %all_to_all.10 = bf16[32,8,896]{2,1,0:T(8,128)(2,1)S(1)} all-to-all(bf16[32,8,896]{2,1,0:T(8,128)(2,1)} %bitcast.46), channel_id=1, replica_groups=mesh['zh'=4,'zl'=4,'y'=8,'x'=4,'c'=2] {'zl','y'}, dimensions={0} | all-to-all | bytes 917504 | tf_op jit(solution)/shard_map/all_to_all | solution.py:84
  27.9 0.1 broadcast_in_dim.8
  28.1 0.0 copy-start
  28.1 26.3 %all_to_all.11 = bf16[4,256,896]{2,1,0:T(8,128)(2,1)S(1)} all-to-all(bf16[4,256,896]{2,1,0:T(8,128)(2,1)S(1)} %broadcast_in_dim.8), channel_id=1, replica_groups=mesh['zh'=4,'zl'=4,'y'=8,'x'=4,'c'=2] {'x'}, dimensions={0} | all-to-all | bytes 3670016 | tf_op jit(solution)/shard_map/all_to_all | solution.py:100
  54.4 5.8 %collective-permute-start.3 = (bf16[1024,896]{1,0:T(8,128)(2,1)S(1)}, bf16[1024,896]{1,0:T(8,128)(2,1)}, u32[]{:S(2)}, u32[]{:S(2)}) collective-permute-start(bf16[1024,896]{1,0:T(8,128)(2,1)S(1)} %bitcast.43), channel_id=1, source_target_pairs={{0,1},{1,0},{2,3},{3,2},{4,5},{5,4},{6,7},{7,6},{8,9},{9,8},{10,11... | collective-permute-start | bytes 5505032 | tf_op jit(solution)/shard_map/ppermute | solution.py:102
  60.2 0.0 copy-done
  60.3 2.8 %collective-permute-start = (bf16[2,4,64,256]{3,2,1,0:T(8,128)(2,1)S(1)}, bf16[2,4,64,256]{3,2,1,0:T(8,128)(2,1)S(1)}, u32[]{:S(2)}, u32[]{:S(2)}) collective-permute-start(bf16[2,4,64,256]{3,2,1,0:T(8,128)(2,1)S(1)} %bitcast.49), channel_id=1, source_target_pairs={{0,64},{64,0},{128,192},{192,128},{1,65},{65,1},{129,193},{193,129... | collective-permute-start | bytes 786440 | tf_op jit(solution)/shard_map/ppermute | solution.py:89
  63.0 5.8 %collective-permute-start.1 = (bf16[2,4,64,256]{3,2,1,0:T(8,128)(2,1)S(1)}, bf16[2,4,64,256]{3,2,1,0:T(8,128)(2,1)S(1)}, u32[]{:S(2)}, u32[]{:S(2)}) collective-permute-start(bf16[2,4,64,256]{3,2,1,0:T(8,128)(2,1)S(1)} %bitcast.50), channel_id=1, source_target_pairs={{0,128},{64,192},{128,0},{192,64},{1,129},{65,193},{129,1},{193,65... | collective-permute-start | bytes 786440 | tf_op jit(solution)/shard_map/ppermute | solution.py:89
  68.8 1.9 %collective-permute-start.2 = (bf16[2,4,64,256]{3,2,1,0:T(8,128)(2,1)S(1)}, bf16[2,4,64,256]{3,2,1,0:T(8,128)(2,1)S(1)}, u32[]{:S(2)}, u32[]{:S(2)}) collective-permute-start(bf16[2,4,64,256]{3,2,1,0:T(8,128)(2,1)S(1)} %bitcast.51), channel_id=1, source_target_pairs={{0,192},{64,128},{128,64},{192,0},{1,193},{65,129},{129,65},{193,1... | collective-permute-start | bytes 786440 | tf_op jit(solution)/shard_map/ppermute | solution.py:89
  70.7 0.0 collective-permute-done
  70.8 15.7 %collective-permute-done.1 = bf16[2,4,64,256]{3,2,1,0:T(8,128)(2,1)S(1)} collective-permute-done((bf16[2,4,64,256]{3,2,1,0:T(8,128)(2,1)S(1)}, bf16[2,4,64,256]{3,2,1,0:T(8,128)(2,1)S(1)}, u32[]{:S(2)}, u32[]{:S(2)}) %collective-permute-start.1) | collective-permute-done | bytes 262176 | tf_op jit(solution)/shard_map/ppermute | solution.py:89
  86.4 0.0 collective-permute-done.2
  86.4 0.1 pad_maximum_fusion
  86.6 0.1 dynamic-slice_bitcast_fusion.3
  86.7 0.1 pad_maximum_fusion.1
  86.8 0.7 fusion.2
  87.5 0.0 collective-permute-done.3
  87.5 2.2 %fusion = bf16[896,256]{1,0:T(8,128)(2,1)S(1)} fusion(f32[896,256]{1,0:T(8,128)S(1)} %fusion.2, bf16[1024,896]{1,0:T(8,128)(2,1)} %collective-permute-done.3, bf16[2,1024,256]{2,1,0:T(8,128)(2,1)S(1)} %bitcast.48, s32[]{:T(128)S(6)} %select_n.38), kind=kOutput, calls=%fused_computation.1 | convolution fusion | flops 470220800 | bytes 3735556 | tf_op jit(solution)/shard_map/dot_general | solution.py:105
  89.8 16.4 %collective-permute-start.4 = (bf16[224,256]{1,0:T(8,128)(2,1)S(1)}, bf16[224,256]{1,0:T(8,128)(2,1)S(1)}, u32[]{:S(2)}, u32[]{:S(2)}) collective-permute-start(bf16[224,256]{1,0:T(8,128)(2,1)S(1)} %get-tuple-element.9), channel_id=1, source_target_pairs={{0,512},{256,768},{512,0},{768,256},{1,513},{257,769},{513,1},{769... | collective-permute-start | bytes 344072 | tf_op jit(solution)/shard_map/ppermute | solution.py:122
  106.2 1.9 %collective-permute-start.5 = (bf16[224,256]{1,0:T(8,128)(2,1)S(1)}, bf16[224,256]{1,0:T(8,128)(2,1)S(1)}, u32[]{:S(2)}, u32[]{:S(2)}) collective-permute-start(bf16[224,256]{1,0:T(8,128)(2,1)S(1)} %get-tuple-element.11), channel_id=1, source_target_pairs={{0,768},{256,512},{512,256},{768,0},{1,769},{257,513},{513,257},{7... | collective-permute-start | bytes 344072 | tf_op jit(solution)/shard_map/ppermute | solution.py:122
  108.1 5.8 %collective-permute-start.6 = (bf16[224,256]{1,0:T(8,128)(2,1)S(1)}, bf16[224,256]{1,0:T(8,128)(2,1)S(1)}, u32[]{:S(2)}, u32[]{:S(2)}) collective-permute-start(bf16[224,256]{1,0:T(8,128)(2,1)S(1)} %get-tuple-element.10), channel_id=1, source_target_pairs={{0,256},{256,0},{512,768},{768,512},{1,257},{257,1},{513,769},{769... | collective-permute-start | bytes 344072 | tf_op jit(solution)/shard_map/ppermute | solution.py:122
  113.9 0.0 collective-permute-done.4
  113.9 8.5 %collective-permute-done.5 = bf16[224,256]{1,0:T(8,128)(2,1)S(1)} collective-permute-done((bf16[224,256]{1,0:T(8,128)(2,1)S(1)}, bf16[224,256]{1,0:T(8,128)(2,1)S(1)}, u32[]{:S(2)}, u32[]{:S(2)}) %collective-permute-start.5) | collective-permute-done | bytes 114720 | tf_op jit(solution)/shard_map/ppermute | solution.py:122
  122.4 5.3 %collective-permute-done.6 = bf16[224,256]{1,0:T(8,128)(2,1)S(1)} collective-permute-done((bf16[224,256]{1,0:T(8,128)(2,1)S(1)}, bf16[224,256]{1,0:T(8,128)(2,1)S(1)}, u32[]{:S(2)}, u32[]{:S(2)}) %collective-permute-start.6) | collective-permute-done | bytes 114720 | tf_op jit(solution)/shard_map/ppermute | solution.py:122
  127.7 0.7 fusion.7
  (2 shorter events, 0.1 us)
Async XLA Ops:
  28.1 32.1 %copy-start = (bf16[512,256]{1,0:T(8,128)(2,1)S(1)}, bf16[512,256]{1,0:T(8,128)(2,1)}, u32[]{:S(2)}) copy-start(bf16[512,256]{1,0:T(8,128)(2,1)} %param.7) | copy-start | bytes 786436
  54.4 33.2 %collective-permute-start.3 = (bf16[1024,896]{1,0:T(8,128)(2,1)S(1)}, bf16[1024,896]{1,0:T(8,128)(2,1)}, u32[]{:S(2)}, u32[]{:S(2)}) collective-permute-start(bf16[1024,896]{1,0:T(8,128)(2,1)S(1)} %bitcast.43), channel_id=1, source_target_pairs={{0,1},{1,0},{2,3},{3,2},{4,5},{5,4},{6,7},{7,6},{8,9},{9,8},{10,11... | collective-permute-start | bytes 5505032 | tf_op jit(solution)/shard_map/ppermute | solution.py:102
  60.3 10.5 %collective-permute-start = (bf16[2,4,64,256]{3,2,1,0:T(8,128)(2,1)S(1)}, bf16[2,4,64,256]{3,2,1,0:T(8,128)(2,1)S(1)}, u32[]{:S(2)}, u32[]{:S(2)}) collective-permute-start(bf16[2,4,64,256]{3,2,1,0:T(8,128)(2,1)S(1)} %bitcast.49), channel_id=1, source_target_pairs={{0,64},{64,0},{128,192},{192,128},{1,65},{65,1},{129,193},{193,129... | collective-permute-start | bytes 786440 | tf_op jit(solution)/shard_map/ppermute | solution.py:89
  63.0 23.4 %collective-permute-start.1 = (bf16[2,4,64,256]{3,2,1,0:T(8,128)(2,1)S(1)}, bf16[2,4,64,256]{3,2,1,0:T(8,128)(2,1)S(1)}, u32[]{:S(2)}, u32[]{:S(2)}) collective-permute-start(bf16[2,4,64,256]{3,2,1,0:T(8,128)(2,1)S(1)} %bitcast.50), channel_id=1, source_target_pairs={{0,128},{64,192},{128,0},{192,64},{1,129},{65,193},{129,1},{193,65... | collective-permute-start | bytes 786440 | tf_op jit(solution)/shard_map/ppermute | solution.py:89
  68.8 17.7 %collective-permute-start.2 = (bf16[2,4,64,256]{3,2,1,0:T(8,128)(2,1)S(1)}, bf16[2,4,64,256]{3,2,1,0:T(8,128)(2,1)S(1)}, u32[]{:S(2)}, u32[]{:S(2)}) collective-permute-start(bf16[2,4,64,256]{3,2,1,0:T(8,128)(2,1)S(1)} %bitcast.51), channel_id=1, source_target_pairs={{0,192},{64,128},{128,64},{192,0},{1,193},{65,129},{129,65},{193,1... | collective-permute-start | bytes 786440 | tf_op jit(solution)/shard_map/ppermute | solution.py:89
  89.8 24.2 %collective-permute-start.4 = (bf16[224,256]{1,0:T(8,128)(2,1)S(1)}, bf16[224,256]{1,0:T(8,128)(2,1)S(1)}, u32[]{:S(2)}, u32[]{:S(2)}) collective-permute-start(bf16[224,256]{1,0:T(8,128)(2,1)S(1)} %get-tuple-element.9), channel_id=1, source_target_pairs={{0,512},{256,768},{512,0},{768,256},{1,513},{257,769},{513,1},{769... | collective-permute-start | bytes 344072 | tf_op jit(solution)/shard_map/ppermute | solution.py:122
  106.2 16.3 %collective-permute-start.5 = (bf16[224,256]{1,0:T(8,128)(2,1)S(1)}, bf16[224,256]{1,0:T(8,128)(2,1)S(1)}, u32[]{:S(2)}, u32[]{:S(2)}) collective-permute-start(bf16[224,256]{1,0:T(8,128)(2,1)S(1)} %get-tuple-element.11), channel_id=1, source_target_pairs={{0,768},{256,512},{512,256},{768,0},{1,769},{257,513},{513,257},{7... | collective-permute-start | bytes 344072 | tf_op jit(solution)/shard_map/ppermute | solution.py:122
  108.1 19.6 %collective-permute-start.6 = (bf16[224,256]{1,0:T(8,128)(2,1)S(1)}, bf16[224,256]{1,0:T(8,128)(2,1)S(1)}, u32[]{:S(2)}, u32[]{:S(2)}) collective-permute-start(bf16[224,256]{1,0:T(8,128)(2,1)S(1)} %get-tuple-element.10), channel_id=1, source_target_pairs={{0,256},{256,0},{512,768},{768,512},{1,257},{257,1},{513,769},{769... | collective-permute-start | bytes 344072 | tf_op jit(solution)/shard_map/ppermute | solution.py:122
where the time goes:
time: 129 us; the launch traced here: 128 us
  blocking collectives  51.8 us (40%)
  starting transfers between devices  40.4 us (31%)
  waiting for transfers between devices  29.5 us (23%)
  matrix products  2.88 us (2%)
  Pallas kernels  2.44 us (2%)
    all_to_all x1, blocking collectives, gradient(): rows = lax.all_to_all(arrived, 'x', split_axis=0, concat_axis=0, tiled=True)  26.3 us
    all_to_all x1, blocking collectives, gradient(): lax.all_to_all(outbound, ('zl', 'y'), split_axis=0, concat_axis=0, tiled=...  25.5 us
    ppermute x3, starting transfers between devices, gradient(): got = lax.ppermute(chunk(step), 'zh', [(i, i ^ step) for i in range(GROUP)])  24.1 us
    ppermute x3, waiting for transfers between devices, gradient(): lax.ppermute(mine, 'zl', [(i, i ^ step) for i in range(GROUP)])  15.7 us
    ppermute x3, waiting for transfers between devices, gradient(): got = lax.ppermute(chunk(step), 'zh', [(i, i ^ step) for i in range(GROUP)])  13.8 us
    ppermute x3, starting transfers between devices, gradient(): lax.ppermute(mine, 'zl', [(i, i ^ step) for i in range(GROUP)])  10.4 us
    ppermute x1, starting transfers between devices, gradient(): others = lax.ppermute(rows, 'c', [(0, 1), (1, 0)])  5.85 us
    dot_general x2, matrix products, product(): lax.dot_general(part, lax.dynamic_index_in_dim(saved, which, 0, False), (...  2.88 us
  transfers between devices with their start and end apart: 7, of which 3 were waited for; matrix products, arithmetic and copies ran while one was open for 1% of the time, Pallas kernels for 0%

commit v1 on v0

--- a/solution.py
+++ b/solution.py
@@ -83,6 +83,10 @@
     outbound = outbound.reshape(GROUP * EXPERTS, CAP, features)
     arrived = lax.all_to_all(outbound, ("zl", "y"), split_axis=0, concat_axis=0, tiled=True)
     mine = hidden.reshape(EXPERTS, GROUP, 2, CAP, columns).transpose(2, 1, 0, 3, 4)
+    mine = jnp.concatenate([mine, mine], axis=0)
+    mine = lax.dynamic_slice_in_dim(mine, core, 2, axis=0)
+    mine = jnp.concatenate([mine, mine], axis=1)
+    mine = lax.dynamic_slice_in_dim(mine, lax.axis_index("x"), GROUP, axis=1)
     mine = mine.reshape(2, GROUP, EXPERTS * CAP, columns)
     gathered = [mine]
     for step in (1, 2, 3):
@@ -92,25 +96,32 @@
         [lax.dynamic_index_in_dim(stacked, low ^ source, 0, False) for source in range(GROUP)],
         axis=2,
     )
-    saved = saved.reshape(2, -1, columns)
+    saved = saved.reshape(2, GROUP, -1, columns)
 
-    arrived = jnp.broadcast_to(
-        arrived.reshape(1, -1, features), (GROUP, GROUP * EXPERTS * CAP, features)
-    )
-    rows = lax.all_to_all(arrived, "x", split_axis=0, concat_axis=0, tiled=True)
-    rows = rows.reshape(-1, features)
-    others = lax.ppermute(rows, "c", [(0, 1), (1, 0)])
+    def from_x(part, step):
+        return lax.ppermute(part, "x", [((i + step) % GROUP, i) for i in range(GROUP)])
+
+    arrived = arrived.reshape(-1, features)
+    half = arrived.shape[0] // 2
+    after, before = from_x(arrived, 1), from_x(arrived, 3)
+    through = after[:half], before[half:]
+    opposite = [from_x(through[0], 1), from_x(through[1], 3)]
+    near = jnp.concatenate([arrived, after, before])
+    far = jnp.concatenate(opposite)
+    swapped = []
+    for part in (near, far):
+        swapped.append(lax.ppermute(part, "c", [(0, 1), (1, 0)]))
 
     def product(part, which):
         return lax.dot_general(
-            part,
-            lax.dynamic_index_in_dim(saved, which, 0, False),
-            (((0,), (0,)), ((), ())),
-            preferred_element_type=jnp.float32,
+            part, which, (((0,), (0,)), ((), ())), preferred_element_type=jnp.float32
         )
 
-    partial = lax.optimization_barrier(product(rows, core))
-    partial = partial + product(others, 1 - core)
+    close = jnp.concatenate([saved[:, :2], saved[:, 3:]], axis=1).reshape(2, -1, columns)
+    partial = product(near, close[0]) + product(far, saved[0, 2])
+    partial = lax.optimization_barrier(partial)
+    partial = lax.optimization_barrier(partial + product(swapped[0], close[1]))
+    partial = partial + product(swapped[1], saved[1, 2])
     partial = partial.astype(jnp.bfloat16).reshape(GROUP, features // GROUP, columns)
     high = lax.axis_index("zh")
 
@@ -118,7 +129,7 @@
         return lax.dynamic_index_in_dim(partial, high ^ step, 0, False)
 
     total = chunk(0).astype(jnp.float32)
-    for step in (2, 3, 1):
+    for step in (3, 2, 1):
         got = lax.ppermute(chunk(step), "zh", [(i, i ^ step) for i in range(GROUP)])
         total = total + got.astype(jnp.float32)
     return total

time: 129 us -> 129 us (level)
  the two profiles are of different devices: /device:TPU:1 before, /device:TPU:8 now
where the time goes in v1:
time: 129 us
  starting transfers between devices  68.1 us (53%)
  waiting for transfers between devices  54 us (42%)
  Pallas kernels  2.49 us (2%)
  matrix products  1.81 us (1%)
  other arithmetic  1.68 us (1%)
    ppermute x3, starting transfers between devices, gradient(): got = lax.ppermute(chunk(step), 'zh', [(i, i ^ step) for i in range(GROUP)])  24.7 us
    ppermute x3, waiting for transfers between devices, gradient(): got = lax.ppermute(chunk(step), 'zh', [(i, i ^ step) for i in range(GROUP)])  17.2 us
    all_to_all x1, starting transfers between devices, gradient(): lax.all_to_all(outbound, ('zl', 'y'), split_axis=0, concat_axis=0, tiled=...  16.6 us
    ppermute x3, waiting for transfers between devices, gradient(): lax.ppermute(mine, 'zl', [(i, i ^ step) for i in range(GROUP)])  15.3 us
    ppermute x4, starting transfers between devices, from_x(): lax.ppermute(part, 'x', [((i + step) % GROUP, i) for i in range(GROUP)])  12.9 us
    all_to_all x1, waiting for transfers between devices, gradient(): lax.all_to_all(outbound, ('zl', 'y'), split_axis=0, concat_axis=0, tiled=...  12.2 us
    ppermute x3, starting transfers between devices, gradient(): lax.ppermute(mine, 'zl', [(i, i ^ step) for i in range(GROUP)])  10.1 us
    ppermute x4, waiting for transfers between devices, from_x(): lax.ppermute(part, 'x', [((i + step) % GROUP, i) for i in range(GROUP)])  8.53 us
  transfers between devices with their start and end apart: 13, of which 7 were waited for; matrix products, arithmetic and copies ran while one was open for 2% of the time, Pallas kernels for 0%

profile of v1, /device:TPU:8, one launch (start us, length us, event | category | flops | bytes accessed | tf_op | source)
XLA Modules:
  0.0 128.7 jit_solution(3708995733480836839)
XLA Ops:
  0.0 2.5 %shard_map.46 = bf16[4,8,8,896]{3,2,1,0:T(8,128)(2,1)} custom-call(bf16[128,3584]{1,0:T(8,128)(2,1)} %grad_in.1, s32[8,128]{1,0:T(8,128)} %bitcast.63, f32[8,128]{1,0:T(8,128)} %bitcast.64), custom_call_target="tpu_custom_call" | custom-call | flops 58720256 | bytes 1376256 | tf_op jit(solution)/shard_map/pallas_call | solution.py:60
  2.5 16.6 %all-to-all-start = ((bf16[32,8,896]{2,1,0:T(8,128)(2,1)}), bf16[32,8,896]{2,1,0:T(8,128)(2,1)S(1)}, u32[]{:S(2)}, u32[]{:S(2)}) async-start(bf16[32,8,896]{2,1,0:T(8,128)(2,1)} %bitcast.56), calls=%async_computation | async-start | bytes 917504 | tf_op jit(solution)/shard_map/all_to_all | solution.py:84
  19.3 12.2 %all-to-all-done = bf16[32,8,896]{2,1,0:T(8,128)(2,1)S(1)} async-done(((bf16[32,8,896]{2,1,0:T(8,128)(2,1)}), bf16[32,8,896]{2,1,0:T(8,128)(2,1)S(1)}, u32[]{:S(2)}, u32[]{:S(2)}) %all-to-all-start) | async-done | bytes 458784 | tf_op jit(solution)/shard_map/all_to_all | solution.py:84
  31.4 3.6 %collective-permute-start.1 = (bf16[256,896]{1,0:T(8,128)(2,1)S(1)}, bf16[256,896]{1,0:T(8,128)(2,1)S(1)}, u32[]{:S(2)}, u32[]{:S(2)}) collective-permute-start(bf16[256,896]{1,0:T(8,128)(2,1)S(1)} %bitcast.50), channel_id=1, source_target_pairs={{6,0},{0,2},{2,4},{4,6},{7,1},{1,3},{3,5},{5,7},{14,8},{8,10},{10,... | collective-permute-start | bytes 1376264 | tf_op jit(solution)/shard_map/ppermute | solution.py:102
  35.1 3.4 %collective-permute-start = (bf16[256,896]{1,0:T(8,128)(2,1)S(1)}, bf16[256,896]{1,0:T(8,128)(2,1)S(1)}, u32[]{:S(2)}, u32[]{:S(2)}) collective-permute-start(bf16[256,896]{1,0:T(8,128)(2,1)S(1)} %bitcast.51), channel_id=1, source_target_pairs={{2,0},{4,2},{6,4},{0,6},{3,1},{5,3},{7,5},{1,7},{10,8},{12,10},{14... | collective-permute-start | bytes 1376264 | tf_op jit(solution)/shard_map/ppermute | solution.py:102
  38.5 0.1 copy_bitcast_fusion.1
  38.6 3.9 %collective-permute-start.4 = (bf16[2,4,64,256]{3,2,1,0:T(8,128)(2,1)S(1)}, bf16[2,4,64,256]{3,2,1,0:T(8,128)(2,1)S(1)}, u32[]{:S(2)}, u32[]{:S(2)}) collective-permute-start(bf16[2,4,64,256]{3,2,1,0:T(8,128)(2,1)S(1)} %get-tuple-element.15), channel_id=1, source_target_pairs={{0,192},{64,128},{128,64},{192,0},{1,193},{65,129},{129,65},{193,1... | collective-permute-start | bytes 786440 | tf_op jit(solution)/shard_map/ppermute | solution.py:93
  42.5 2.5 %collective-permute-start.3 = (bf16[2,4,64,256]{3,2,1,0:T(8,128)(2,1)S(1)}, bf16[2,4,64,256]{3,2,1,0:T(8,128)(2,1)S(1)}, u32[]{:S(2)}, u32[]{:S(2)}) collective-permute-start(bf16[2,4,64,256]{3,2,1,0:T(8,128)(2,1)S(1)} %get-tuple-element.15), channel_id=1, source_target_pairs={{0,128},{64,192},{128,0},{192,64},{1,129},{65,193},{129,1},{193,65... | collective-permute-start | bytes 786440 | tf_op jit(solution)/shard_map/ppermute | solution.py:93
  45.1 3.7 %collective-permute-start.2 = (bf16[2,4,64,256]{3,2,1,0:T(8,128)(2,1)S(1)}, bf16[2,4,64,256]{3,2,1,0:T(8,128)(2,1)S(1)}, u32[]{:S(2)}, u32[]{:S(2)}) collective-permute-start(bf16[2,4,64,256]{3,2,1,0:T(8,128)(2,1)S(1)} %get-tuple-element.15), channel_id=1, source_target_pairs={{0,64},{64,0},{128,192},{192,128},{1,65},{65,1},{129,193},{193,129... | collective-permute-start | bytes 786440 | tf_op jit(solution)/shard_map/ppermute | solution.py:93
  48.8 2.5 %collective-permute-done.4 = bf16[2,4,64,256]{3,2,1,0:T(8,128)(2,1)S(1)} collective-permute-done((bf16[2,4,64,256]{3,2,1,0:T(8,128)(2,1)S(1)}, bf16[2,4,64,256]{3,2,1,0:T(8,128)(2,1)S(1)}, u32[]{:S(2)}, u32[]{:S(2)}) %collective-permute-start.4) | collective-permute-done | bytes 262176 | tf_op jit(solution)/shard_map/ppermute | solution.py:93
  51.3 12.8 %collective-permute-done.3 = bf16[2,4,64,256]{3,2,1,0:T(8,128)(2,1)S(1)} collective-permute-done((bf16[2,4,64,256]{3,2,1,0:T(8,128)(2,1)S(1)}, bf16[2,4,64,256]{3,2,1,0:T(8,128)(2,1)S(1)}, u32[]{:S(2)}, u32[]{:S(2)}) %collective-permute-start.3) | collective-permute-done | bytes 262176 | tf_op jit(solution)/shard_map/ppermute | solution.py:93
  64.1 0.1 pad_maximum_fusion.1
  64.2 0.1 pad_maximum_fusion
  64.4 1.9 %collective-permute-start.7 = (bf16[768,896]{1,0:T(8,128)(2,1)S(1)}, bf16[768,896]{1,0:T(8,128)(2,1)S(1)}, u32[]{:S(2)}, u32[]{:S(2)}) collective-permute-start(bf16[768,896]{1,0:T(8,128)(2,1)S(1)} %pad_maximum_fusion), channel_id=1, source_target_pairs={{0,1},{1,0},{2,3},{3,2},{4,5},{5,4},{6,7},{7,6},{8,9},{9,8},{10,11... | collective-permute-start | bytes 4128776 | tf_op jit(solution)/shard_map/ppermute | solution.py:113
  66.4 3.6 %collective-permute-start.5 = (bf16[128,896]{1,0:T(8,128)(2,1)S(1)}, bf16[128,896]{1,0:T(8,128)(2,1)S(1)}, u32[]{:S(2)}, u32[]{:S(2)}) collective-permute-start(bf16[128,896]{1,0:T(8,128)(2,1)S(1)} %slice.38), channel_id=1, source_target_pairs={{2,0},{4,2},{6,4},{0,6},{3,1},{5,3},{7,5},{1,7},{10,8},{12,10},{14... | collective-permute-start | bytes 688136 | tf_op jit(solution)/shard_map/ppermute | solution.py:102
  70.1 0.1 pad_maximum_fusion.2
  70.3 2.2 %collective-permute-start.6 = (bf16[128,896]{1,0:T(8,128)(2,1)S(1)}, bf16[128,896]{1,0:T(8,128)(2,1)S(1)}, u32[]{:S(2)}, u32[]{:S(2)}) collective-permute-start(bf16[128,896]{1,0:T(8,128)(2,1)S(1)} %slice.39), channel_id=1, source_target_pairs={{6,0},{0,2},{2,4},{4,6},{7,1},{1,3},{3,5},{5,7},{14,8},{8,10},{10,... | collective-permute-start | bytes 688136 | tf_op jit(solution)/shard_map/ppermute | solution.py:102
  72.6 3.7 %collective-permute-done.5 = bf16[128,896]{1,0:T(8,128)(2,1)S(1)} collective-permute-done((bf16[128,896]{1,0:T(8,128)(2,1)S(1)}, bf16[128,896]{1,0:T(8,128)(2,1)S(1)}, u32[]{:S(2)}, u32[]{:S(2)}) %collective-permute-start.5) | collective-permute-done | bytes 229408 | tf_op jit(solution)/shard_map/ppermute | solution.py:102
  76.3 4.8 %collective-permute-done.6 = bf16[128,896]{1,0:T(8,128)(2,1)S(1)} collective-permute-done((bf16[128,896]{1,0:T(8,128)(2,1)S(1)}, bf16[128,896]{1,0:T(8,128)(2,1)S(1)}, u32[]{:S(2)}, u32[]{:S(2)}) %collective-permute-start.6) | collective-permute-done | bytes 229408 | tf_op jit(solution)/shard_map/ppermute | solution.py:102
  81.2 1.9 %collective-permute-start.8 = (bf16[256,896]{1,0:T(8,128)(2,1)S(1)}, bf16[256,896]{1,0:T(8,128)(2,1)S(1)}, u32[]{:S(2)}, u32[]{:S(2)}) collective-permute-start(bf16[256,896]{1,0:T(8,128)(2,1)S(1)} %constant_dynamic-update-slice_fusion), channel_id=1, source_target_pairs={{0,1},{1,0},{2,3},{3,2},{4,5},{5,4},{6,7},{7,6},{8,9},{9,8},{10,11... | collective-permute-start | bytes 1376264 | tf_op jit(solution)/shard_map/ppermute | solution.py:113
  83.1 0.3 fusion.6
  83.4 0.6 convolution_add_fusion
  84.0 0.9 collective-permute-done.8
  84.9 0.3 fusion.5
  85.2 0.6 fusion.7
  85.8 0.1 add.57
  85.9 0.1 add_convert_fusion
  86.1 15.5 %collective-permute-start.9 = (bf16[224,256]{1,0:T(8,128)(2,1)S(1)}, bf16[224,256]{1,0:T(8,128)(2,1)S(1)}, u32[]{:S(2)}, u32[]{:S(2)}) collective-permute-start(bf16[224,256]{1,0:T(8,128)(2,1)S(1)} %get-tuple-element.11), channel_id=1, source_target_pairs={{0,768},{256,512},{512,256},{768,0},{1,769},{257,513},{513,257},{7... | collective-permute-start | bytes 344072 | tf_op jit(solution)/shard_map/ppermute | solution.py:133
  101.6 3.6 %collective-permute-start.11 = (bf16[224,256]{1,0:T(8,128)(2,1)S(1)}, bf16[224,256]{1,0:T(8,128)(2,1)S(1)}, u32[]{:S(2)}, u32[]{:S(2)}) collective-permute-start(bf16[224,256]{1,0:T(8,128)(2,1)S(1)} %get-tuple-element.12), channel_id=1, source_target_pairs={{0,256},{256,0},{512,768},{768,512},{1,257},{257,1},{513,769},{769... | collective-permute-start | bytes 344072 | tf_op jit(solution)/shard_map/ppermute | solution.py:133
  105.3 5.6 %collective-permute-start.10 = (bf16[224,256]{1,0:T(8,128)(2,1)S(1)}, bf16[224,256]{1,0:T(8,128)(2,1)S(1)}, u32[]{:S(2)}, u32[]{:S(2)}) collective-permute-start(bf16[224,256]{1,0:T(8,128)(2,1)S(1)} %get-tuple-element.13), channel_id=1, source_target_pairs={{0,512},{256,768},{512,0},{768,256},{1,513},{257,769},{513,1},{769... | collective-permute-start | bytes 344072 | tf_op jit(solution)/shard_map/ppermute | solution.py:133
  110.8 17.1 %collective-permute-done.11 = bf16[224,256]{1,0:T(8,128)(2,1)S(1)} collective-permute-done((bf16[224,256]{1,0:T(8,128)(2,1)S(1)}, bf16[224,256]{1,0:T(8,128)(2,1)S(1)}, u32[]{:S(2)}, u32[]{:S(2)}) %collective-permute-start.11) | collective-permute-done | bytes 114720 | tf_op jit(solution)/shard_map/ppermute | solution.py:133
  128.0 0.7 fusion.4
  (18 shorter events, 0.5 us)
Async XLA Ops:
  0.0 19.1 %copy-start = (bf16[512,256]{1,0:T(8,128)(2,1)S(1)}, bf16[512,256]{1,0:T(8,128)(2,1)}, u32[]{:S(2)}) copy-start(bf16[512,256]{1,0:T(8,128)(2,1)} %param.7) | copy-start | bytes 786436
  2.5 28.9 %all-to-all-start = ((bf16[32,8,896]{2,1,0:T(8,128)(2,1)}), bf16[32,8,896]{2,1,0:T(8,128)(2,1)S(1)}, u32[]{:S(2)}, u32[]{:S(2)}) async-start(bf16[32,8,896]{2,1,0:T(8,128)(2,1)} %bitcast.56), calls=%async_computation | async-start | bytes 917504 | tf_op jit(solution)/shard_map/all_to_all | solution.py:84
  31.4 32.8 %collective-permute-start.1 = (bf16[256,896]{1,0:T(8,128)(2,1)S(1)}, bf16[256,896]{1,0:T(8,128)(2,1)S(1)}, u32[]{:S(2)}, u32[]{:S(2)}) collective-permute-start(bf16[256,896]{1,0:T(8,128)(2,1)S(1)} %bitcast.50), channel_id=1, source_target_pairs={{6,0},{0,2},{2,4},{4,6},{7,1},{1,3},{3,5},{5,7},{14,8},{8,10},{10,... | collective-permute-start | bytes 1376264 | tf_op jit(solution)/shard_map/ppermute | solution.py:102
  35.1 29.2 %collective-permute-start = (bf16[256,896]{1,0:T(8,128)(2,1)S(1)}, bf16[256,896]{1,0:T(8,128)(2,1)S(1)}, u32[]{:S(2)}, u32[]{:S(2)}) collective-permute-start(bf16[256,896]{1,0:T(8,128)(2,1)S(1)} %bitcast.51), channel_id=1, source_target_pairs={{2,0},{4,2},{6,4},{0,6},{3,1},{5,3},{7,5},{1,7},{10,8},{12,10},{14... | collective-permute-start | bytes 1376264 | tf_op jit(solution)/shard_map/ppermute | solution.py:102
  38.6 12.7 %collective-permute-start.4 = (bf16[2,4,64,256]{3,2,1,0:T(8,128)(2,1)S(1)}, bf16[2,4,64,256]{3,2,1,0:T(8,128)(2,1)S(1)}, u32[]{:S(2)}, u32[]{:S(2)}) collective-permute-start(bf16[2,4,64,256]{3,2,1,0:T(8,128)(2,1)S(1)} %get-tuple-element.15), channel_id=1, source_target_pairs={{0,192},{64,128},{128,64},{192,0},{1,193},{65,129},{129,65},{193,1... | collective-permute-start | bytes 786440 | tf_op jit(solution)/shard_map/ppermute | solution.py:93
  42.5 21.5 %collective-permute-start.3 = (bf16[2,4,64,256]{3,2,1,0:T(8,128)(2,1)S(1)}, bf16[2,4,64,256]{3,2,1,0:T(8,128)(2,1)S(1)}, u32[]{:S(2)}, u32[]{:S(2)}) collective-permute-start(bf16[2,4,64,256]{3,2,1,0:T(8,128)(2,1)S(1)} %get-tuple-element.15), channel_id=1, source_target_pairs={{0,128},{64,192},{128,0},{192,64},{1,129},{65,193},{129,1},{193,65... | collective-permute-start | bytes 786440 | tf_op jit(solution)/shard_map/ppermute | solution.py:93
  45.1 19.0 %collective-permute-start.2 = (bf16[2,4,64,256]{3,2,1,0:T(8,128)(2,1)S(1)}, bf16[2,4,64,256]{3,2,1,0:T(8,128)(2,1)S(1)}, u32[]{:S(2)}, u32[]{:S(2)}) collective-permute-start(bf16[2,4,64,256]{3,2,1,0:T(8,128)(2,1)S(1)} %get-tuple-element.15), channel_id=1, source_target_pairs={{0,64},{64,0},{128,192},{192,128},{1,65},{65,1},{129,193},{193,129... | collective-permute-start | bytes 786440 | tf_op jit(solution)/shard_map/ppermute | solution.py:93
  64.4 20.8 %collective-permute-start.7 = (bf16[768,896]{1,0:T(8,128)(2,1)S(1)}, bf16[768,896]{1,0:T(8,128)(2,1)S(1)}, u32[]{:S(2)}, u32[]{:S(2)}) collective-permute-start(bf16[768,896]{1,0:T(8,128)(2,1)S(1)} %pad_maximum_fusion), channel_id=1, source_target_pairs={{0,1},{1,0},{2,3},{3,2},{4,5},{5,4},{6,7},{7,6},{8,9},{9,8},{10,11... | collective-permute-start | bytes 4128776 | tf_op jit(solution)/shard_map/ppermute | solution.py:113
  66.4 9.9 %collective-permute-start.5 = (bf16[128,896]{1,0:T(8,128)(2,1)S(1)}, bf16[128,896]{1,0:T(8,128)(2,1)S(1)}, u32[]{:S(2)}, u32[]{:S(2)}) collective-permute-start(bf16[128,896]{1,0:T(8,128)(2,1)S(1)} %slice.38), channel_id=1, source_target_pairs={{2,0},{4,2},{6,4},{0,6},{3,1},{5,3},{7,5},{1,7},{10,8},{12,10},{14... | collective-permute-start | bytes 688136 | tf_op jit(solution)/shard_map/ppermute | solution.py:102
  70.3 10.8 %collective-permute-start.6 = (bf16[128,896]{1,0:T(8,128)(2,1)S(1)}, bf16[128,896]{1,0:T(8,128)(2,1)S(1)}, u32[]{:S(2)}, u32[]{:S(2)}) collective-permute-start(bf16[128,896]{1,0:T(8,128)(2,1)S(1)} %slice.39), channel_id=1, source_target_pairs={{6,0},{0,2},{2,4},{4,6},{7,1},{1,3},{3,5},{5,7},{14,8},{8,10},{10,... | collective-permute-start | bytes 688136 | tf_op jit(solution)/shard_map/ppermute | solution.py:102
  81.2 3.7 %collective-permute-start.8 = (bf16[256,896]{1,0:T(8,128)(2,1)S(1)}, bf16[256,896]{1,0:T(8,128)(2,1)S(1)}, u32[]{:S(2)}, u32[]{:S(2)}) collective-permute-start(bf16[256,896]{1,0:T(8,128)(2,1)S(1)} %constant_dynamic-update-slice_fusion), channel_id=1, source_target_pairs={{0,1},{1,0},{2,3},{3,2},{4,5},{5,4},{6,7},{7,6},{8,9},{9,8},{10,11... | collective-permute-start | bytes 1376264 | tf_op jit(solution)/shard_map/ppermute | solution.py:113
  86.1 24.7 %collective-permute-start.9 = (bf16[224,256]{1,0:T(8,128)(2,1)S(1)}, bf16[224,256]{1,0:T(8,128)(2,1)S(1)}, u32[]{:S(2)}, u32[]{:S(2)}) collective-permute-start(bf16[224,256]{1,0:T(8,128)(2,1)S(1)} %get-tuple-element.11), channel_id=1, source_target_pairs={{0,768},{256,512},{512,256},{768,0},{1,769},{257,513},{513,257},{7... | collective-permute-start | bytes 344072 | tf_op jit(solution)/shard_map/ppermute | solution.py:133
  101.6 26.4 %collective-permute-start.11 = (bf16[224,256]{1,0:T(8,128)(2,1)S(1)}, bf16[224,256]{1,0:T(8,128)(2,1)S(1)}, u32[]{:S(2)}, u32[]{:S(2)}) collective-permute-start(bf16[224,256]{1,0:T(8,128)(2,1)S(1)} %get-tuple-element.12), channel_id=1, source_target_pairs={{0,256},{256,0},{512,768},{768,512},{1,257},{257,1},{513,769},{769... | collective-permute-start | bytes 344072 | tf_op jit(solution)/shard_map/ppermute | solution.py:133
  105.3 22.7 %collective-permute-start.10 = (bf16[224,256]{1,0:T(8,128)(2,1)S(1)}, bf16[224,256]{1,0:T(8,128)(2,1)S(1)}, u32[]{:S(2)}, u32[]{:S(2)}) collective-permute-start(bf16[224,256]{1,0:T(8,128)(2,1)S(1)} %get-tuple-element.13), channel_id=1, source_target_pairs={{0,512},{256,768},{512,0},{768,256},{1,513},{257,769},{513,1},{769... | collective-permute-start | bytes 344072 | tf_op jit(solution)/shard_map/ppermute | solution.py:133
